TPU v7x, 32 devices: a whole 2x2x4 slice. The times are simulated.
32 devices in a mesh: rep: 4 (over z), tp: 8 (over y, x, core).
Axes of the slice: x: 2, y: 2, z: 4, core: 2. Of those that a mesh axis runs over, the one named last changes fastest.
Arguments:
- exp_hidden: bfloat16 [256, 8192], P('rep', 'tp'), may hold values from -160 to 160
- exp_pre_gain: float32 [8192], P('tp'), may hold values from 0.25 to 1.75
- exp_gate: bfloat16 [8192, 28672], P('tp', 'rep'), may hold values from -0.0625 to 0.0625
- exp_up: bfloat16 [8192, 28672], P('tp', 'rep'), may hold values from -0.0625 to 0.0625
- exp_down: bfloat16 [28672, 8192], P('rep', 'tp'), may hold values from -0.03125 to 0.03125
- exp_out_gain: float32 [8192], P('tp'), may hold values from 0.25 to 1.75
- exp_head: bfloat16 [8192, 65536], P(None, ('rep', 'tp')), may hold values from -10 to 10
- ama_hidden: bfloat16 [256, 4096], P('rep', 'tp'), may hold values from -160 to 160
- ama_out_gain: float32 [4096], P('tp'), may hold values from 0.25 to 1.75
- ama_head: bfloat16 [4096, 65536], P(None, ('rep', 'tp')), may hold values from -10 to 10
- logit_scale: float32 [256], replicated, may hold values from 0.25 to 3
- prompt_of: int32 [256], replicated, may hold values from 0 to 7
- prior_picks: int32 [8, 24], replicated, may hold values from 0 to 65535
- valid_mask: int32 [65536], P(('rep', 'tp')), may hold values 0 or 1
Outputs:
- scores: float32 [256, 65536], P(None, ('rep', 'tp'))
- beam_best: float32 [256], replicated
All inputs are finite; a program needn't handle non-finite values. No bound on the sum of `valid_mask` on one device may be relied on, other than what follows from the above.
Results may differ from a plain program's by a relative error of at most 0.0034.
Values may be sent and summed in bfloat16 or wider, within the bound.
No kernel may reach another device: no remote copies, remote signals or barrier semaphores. Data moves between devices by JAX's collectives and lax.ppermute only.
A program may use at most 192 MiB of HBM per device.

v0:
```python
import jax
import jax.numpy as jnp
from jax import lax
from jax.sharding import PartitionSpec as P

DE = 8192
DA = 4096
norm_epsilon = 1e-05
contrast_weight = 0.5
hamming_weight = 0.7


def scaled_rows(values, squares, width, gain):
    return (values * lax.rsqrt(squares[:, None] / width + norm_epsilon) * gain).astype(jnp.bfloat16)


def both_halves(rows_in, gate_weight, up_weight):
    gate = jnp.dot(rows_in, gate_weight, preferred_element_type=jnp.float32)
    up = jnp.dot(rows_in, up_weight, preferred_element_type=jnp.float32)
    return jnp.concatenate([gate, up], axis=1)


def gated_rows(summed, width):
    return (jax.nn.silu(summed[:, :width]) * summed[:, width:]).astype(jnp.bfloat16)


def body(
    exp_hidden,
    exp_pre_gain,
    exp_gate,
    exp_up,
    exp_down,
    exp_out_gain,
    exp_head,
    ama_hidden,
    ama_out_gain,
    ama_head,
    logit_scale,
    prompt_of,
    prior_picks,
    valid_mask,
):
    values_exp = exp_hidden.astype(jnp.float32)
    values_ama = ama_hidden.astype(jnp.float32)
    squares_exp = lax.psum(jnp.sum(values_exp * values_exp, axis=1), "tp")
    normed_exp = scaled_rows(values_exp, squares_exp, DE, exp_pre_gain)
    rows_exp = lax.all_gather(normed_exp, "rep", axis=0, tiled=True)
    width_exp = exp_gate.shape[1]
    summed_exp = lax.psum_scatter(
        both_halves(rows_exp, exp_gate, exp_up), "tp", scatter_dimension=0, tiled=True
    )
    hidden_exp = gated_rows(summed_exp, width_exp)
    term_exp = jnp.dot(
        lax.all_gather(hidden_exp, "tp", axis=0, tiled=True),
        exp_down,
        preferred_element_type=jnp.float32,
    )
    out_exp = lax.psum_scatter(term_exp, "rep", scatter_dimension=0, tiled=True)
    layer_exp = values_exp + out_exp
    final_sq_exp, final_sq_ama = lax.psum(
        (jnp.sum(layer_exp * layer_exp, axis=1), jnp.sum(values_ama * values_ama, axis=1)), "tp"
    )
    final_exp = scaled_rows(layer_exp, final_sq_exp, DE, exp_out_gain)
    final_ama = scaled_rows(values_ama, final_sq_ama, DA, ama_out_gain)
    features_exp, features_ama = (
        lax.all_gather(final_exp, "tp", axis=1, tiled=True),
        lax.all_gather(final_ama, "tp", axis=1, tiled=True),
    )
    full_exp, full_ama = (
        lax.all_gather(features_exp, "rep", axis=0, tiled=True),
        lax.all_gather(features_ama, "rep", axis=0, tiled=True),
    )
    logits_exp = logit_scale[:, None] * jnp.dot(
        full_exp, exp_head, preferred_element_type=jnp.float32
    )
    logits_ama = logit_scale[:, None] * jnp.dot(
        full_ama, ama_head, preferred_element_type=jnp.float32
    )
    top_exp, top_ama = lax.pmax(
        (jnp.max(logits_exp, axis=1), jnp.max(logits_ama, axis=1)), ("rep", "tp")
    )
    local_exp = jnp.sum(jnp.exp(logits_exp - top_exp[:, None]), axis=1)
    local_ama = jnp.sum(jnp.exp(logits_ama - top_ama[:, None]), axis=1)
    total_exp, total_ama = lax.psum((local_exp, local_ama), ("rep", "tp"))
    logp_exp = logits_exp - top_exp[:, None] - jnp.log(total_exp)[:, None]
    logp_ama = logits_ama - top_ama[:, None] - jnp.log(total_ama)[:, None]
    entries = exp_head.shape[1]
    first_entry = lax.axis_index(("rep", "tp")) * entries
    vocab_ids = first_entry + jnp.arange(entries, dtype=jnp.int32)
    picks_row = jnp.take(prior_picks, prompt_of, axis=0)
    counts = jnp.sum(
        (picks_row[:, :, None] == vocab_ids[None, None, :]).astype(jnp.float32), axis=1
    )
    valid = valid_mask.astype(jnp.float32)[None, :]
    scores = logp_exp - contrast_weight * valid * logp_ama - hamming_weight * counts
    beam_best = lax.pmax(jnp.max(scores, axis=1), ("rep", "tp"))
    return (scores, beam_best)


def solution(mesh):
    placed = (
        P("rep", "tp"),
        P("tp"),
        P("tp", "rep"),
        P("tp", "rep"),
        P("rep", "tp"),
        P("tp"),
        P(None, ("rep", "tp")),
        P("rep", "tp"),
        P("tp"),
        P(None, ("rep", "tp")),
        P(),
        P(),
        P(),
        P(("rep", "tp")),
    )
    return jax.shard_map(
        body, mesh=mesh, in_specs=placed, out_specs=(P(None, ("rep", "tp")), P()), check_vma=False
    )
```

profile of v0, /device:TPU:0, one launch (start us, length us, event | category | flops | bytes accessed | tf_op | source)
XLA Modules:
  0.0 552.7 jit_solution(7237676692740054795)
XLA Ops:
  7.2 0.0 copy-start
  7.2 0.0 reduce-scatter.3.cloned.1.call-start
  7.2 1.0 fusion.1
  8.3 15.2 %psum.35 = f32[64]{0:T(128)S(1)} all-reduce(f32[64]{0:T(128)S(1)} %fusion.1), channel_id=1, replica_groups=mesh['rep'=4,'tp'=8] {'tp'}, use_global_device_ids=true, to_apply=%region_1.0 | all-reduce | flops 64 | bytes 512 | tf_op jit(solution)/shard_map/psum | solution.py:45
  23.4 1.0 fusion.3
  24.4 15.9 %all_gather.18 = bf16[256,1024]{1,0:T(8,128)(2,1)S(1)} all-gather(bf16[64,1024]{1,0:T(8,128)(2,1)S(1)} %fusion.3), channel_id=1, replica_groups=mesh['rep'=4,'tp'=8] {'rep'}, dimensions={0}, use_global_device_ids=true | all-gather | bytes 655360 | tf_op jit(solution)/shard_map/all_gather | solution.py:47
  40.4 7.4 %fusion.10 = f32[256,7168]{1,0:T(8,128)S(1)} fusion(bf16[256,1024]{1,0:T(8,128)(2,1)S(1)} %all_gather.18, bf16[1024,7168]{1,0:T(8,128)(2,1)} %param.16), kind=kOutput, calls=%fused_computation.35 | convolution fusion | flops 3758096384 | bytes 22544384 | tf_op jit(solution)/shard_map/dot_general | solution.py:18
  47.8 1.9 copy-done.2
  49.7 4.1 fusion.11
  53.8 5.5 pad_maximum_fusion
  59.3 0.0 reduce-scatter.3.cloned.1.call-update
  59.3 0.0 all-gather.5.cloned.1.call-start
  59.3 103.7 %reduce-scatter.3.cloned.1.call-done = f32[32,14336]{1,0:T(8,128)} async-done(((f32[256,14336]{1,0:T(8,128)}), f32[32,14336]{1,0:T(8,128)}) %reduce-scatter.3.cloned.1.call-update) | async-done | bytes 1835024 | tf_op jit(solution)/shard_map/reduce_scatter | solution.py:49
  163.1 2.5 fusion
  165.6 0.0 all-gather.5.cloned.1.call-update
  165.6 0.0 copy-start.6
  165.6 0.0 copy-start.7
  165.6 0.0 reduce-scatter.5.cloned.1.call-start
  165.7 34.4 %all-gather.5.cloned.1.call-done = bf16[256,7168]{1,0:T(8,128)(2,1)} async-done(((bf16[32,7168]{1,0:T(8,128)(2,1)}), bf16[256,7168]{1,0:T(8,128)(2,1)}) %all-gather.5.cloned.1.call-update) | async-done | bytes 3670032 | tf_op jit(solution)/shard_map/all_gather | solution.py:54
  200.1 11.2 %fusion.12 = f32[256,1024]{1,0:T(8,128)} fusion(bf16[256,7168]{1,0:T(8,128)(2,1)} %all-gather.5.cloned.1.call-done, bf16[7168,1024]{1,0:T(8,128)(2,1)} %param.18), kind=kOutput, calls=%fused_computation.37 | convolution fusion | flops 3758096384 | bytes 19398656 | tf_op jit(solution)/shard_map/dot_general | solution.py:53
  211.3 0.0 reduce-scatter.5.cloned.1.call-update
  211.4 0.0 copy-start.9
  211.4 0.0 all-gather.7.cloned.1.call-start
  211.4 0.1 fusion.4
  211.5 27.3 %reduce-scatter.5.cloned.1.call-done = f32[64,1024]{1,0:T(8,128)} async-done(((f32[256,1024]{1,0:T(8,128)}), f32[64,1024]{1,0:T(8,128)}) %reduce-scatter.5.cloned.1.call-update) | async-done | bytes 262160 | tf_op jit(solution)/shard_map/reduce_scatter | solution.py:58
  238.8 1.1 multiply_reduce_fusion
  239.9 13.2 %all-reduce.2 = (f32[64]{0:T(128)S(1)}, f32[64]{0:T(128)S(1)}) all-reduce(f32[64]{0:T(128)S(1)} %fusion.4, f32[64]{0:T(128)S(1)} %multiply_reduce_fusion), channel_id=1, replica_groups=mesh['rep'=4,'tp'=8] {'tp'}, use_global_device_ids=true, to_apply=%region_11.12 | all-reduce | flops 128 | bytes 1024 | tf_op jit(solution)/shard_map/psum | solution.py:60
  253.1 1.7 multiply_convert_fusion
  254.8 0.0 all-gather.7.cloned.1.call-update
  254.8 0.0 all-gather.11.cloned.1.call-start
  254.9 0.1 fusion.6
  255.0 10.5 %all_gather.22 = bf16[64,4096]{1,0:T(8,128)(2,1)} all-gather(bf16[64,512]{1,0:T(8,128)(2,1)S(1)} %fusion.6), channel_id=1, replica_groups=mesh['rep'=4,'tp'=8] {'tp'}, dimensions={1}, use_global_device_ids=true | all-gather | bytes 589824 | tf_op jit(solution)/shard_map/all_gather | solution.py:67
  265.5 0.0 all-gather.11.cloned.1.call-update
  265.6 0.2 all-gather.9.cloned.1.call-start
  265.8 9.6 %all-gather.7.cloned.1.call-done = bf16[64,8192]{1,0:T(8,128)(2,1)} async-done(((bf16[64,1024]{1,0:T(8,128)(2,1)}), bf16[64,8192]{1,0:T(8,128)(2,1)}) %all-gather.7.cloned.1.call-update) | async-done | bytes 1048592 | tf_op jit(solution)/shard_map/all_gather | solution.py:66
  275.4 0.0 all-gather.9.cloned.1.call-update
  275.5 0.7 gather_fusion
  276.3 0.1 broadcast_select_fusion
  276.4 20.6 %convert_reduce_fusion = f32[256,2048]{1,0:T(8,128)} fusion(s32[2048]{0:T(1024)S(1)} %iota_add_fusion, s32[256,24]{1,0:T(8,128)S(1)} %broadcast_select_fusion), kind=kLoop, calls=%fused_computation.1 | loop fusion | flops 37224448 | bytes 2129920 | tf_op jit(solution)/shard_map/reduce_sum | solution.py:91
  297.0 25.5 %all-gather.11.cloned.1.call-done = bf16[256,4096]{1,0:T(8,128)(2,1)} async-done(((bf16[64,4096]{1,0:T(8,128)(2,1)}), bf16[256,4096]{1,0:T(8,128)(2,1)}) %all-gather.11.cloned.1.call-update) | async-done | bytes 2097168 | tf_op jit(solution)/shard_map/all_gather | solution.py:71
  322.5 8.8 %fusion.8 = (f32[256]{0:T(256)S(1)}, f32[256,2048]{1,0:T(8,128)S(1)}) fusion(bf16[256,4096]{1,0:T(8,128)(2,1)} %all-gather.11.cloned.1.call-done, bf16[4096,2048]{1,0:T(8,128)(2,1)} %param.23, f32[256]{0:T(256)S(1)} %copy-done.9), kind=kOutput, calls=%fused_computation.33 | convolution fusion | flops 4296015872 | bytes 20973568 | tf_op jit(solution)/shard_map/dot_general | solution.py:76
  331.3 72.2 %all-gather.9.cloned.1.call-done = bf16[256,8192]{1,0:T(8,128)(2,1)} async-done(((bf16[64,8192]{1,0:T(8,128)(2,1)}), bf16[256,8192]{1,0:T(8,128)(2,1)}) %all-gather.9.cloned.1.call-update) | async-done | bytes 4194320 | tf_op jit(solution)/shard_map/all_gather | solution.py:70
  403.5 17.2 %fusion.9 = (f32[256]{0:T(256)S(1)}, f32[256,2048]{1,0:T(8,128)}) fusion(bf16[256,8192]{1,0:T(8,128)(2,1)} %all-gather.9.cloned.1.call-done, bf16[8192,2048]{1,0:T(8,128)(2,1)} %param.20, f32[256]{0:T(256)S(1)} %copy-done.9), kind=kOutput, calls=%fused_computation.34 | convolution fusion | flops 8590983168 | bytes 39847936 | tf_op jit(solution)/shard_map/dot_general | solution.py:73
  420.7 38.6 %all-reduce.1 = (f32[256]{0:T(256)S(1)}, f32[256]{0:T(256)S(1)}) all-reduce(f32[256]{0:T(256)S(1)} %get-tuple-element.10, f32[256]{0:T(256)S(1)} %get-tuple-element.12), channel_id=1, replica_groups=mesh['rep'=4,'tp'=8] {'rep','tp'}, use_global_device_ids=true, to_apply=%region_13.14 | all-reduce | flops 512 | bytes 4096 | tf_op jit(solution)/shard_map/pmax | solution.py:79
  459.4 2.3 exponential_reduce_fusion
  461.7 40.4 %all-reduce = (f32[256]{0:T(256)S(1)}, f32[256]{0:T(256)S(1)}) all-reduce(f32[256]{0:T(256)S(1)} %get-tuple-element.14, f32[256]{0:T(256)S(1)} %get-tuple-element.15), channel_id=1, replica_groups=mesh['rep'=4,'tp'=8] {'rep','tp'}, use_global_device_ids=true, to_apply=%region_15.16 | all-reduce | flops 512 | bytes 4096 | tf_op jit(solution)/shard_map/psum | solution.py:84
  502.1 4.4 fusion.7
  506.5 39.4 %pmax.23 = f32[256]{0:T(256)} all-reduce(f32[256]{0:T(256)S(1)} %get-tuple-element.8), channel_id=1, replica_groups=mesh['rep'=4,'tp'=8] {'rep','tp'}, use_global_device_ids=true, to_apply=%region_18.19 | all-reduce | flops 256 | bytes 2048 | tf_op jit(solution)/shard_map/pmax | solution.py:96
  (25 shorter events, 0.1 us)
Async XLA Ops:
  7.2 268.3 %copy-start = (s32[8,24]{1,0:T(8,128)S(1)}, s32[8,24]{1,0:T(8,128)}, u32[]{:S(2)}) copy-start(s32[8,24]{1,0:T(8,128)} %param.26) | copy-start | bytes 2308
  7.2 155.9 %reduce-scatter.3.cloned.1.call-start = ((), (), s32[]{:S(2)}) async-start(), calls=%async_computation.2 | async-start | bytes 16515072 | tf_op jit(solution)/shard_map/reduce_scatter | solution.py:49
  40.4 9.3 %copy-start.2 = (bf16[1024,7168]{1,0:T(8,128)(2,1)S(1)}, bf16[1024,7168]{1,0:T(8,128)(2,1)}, u32[]{:S(2)}) copy-start(bf16[1024,7168]{1,0:T(8,128)(2,1)} %param.17) | copy-start | bytes 44040196
  59.3 140.8 %all-gather.5.cloned.1.call-start = ((), (), s32[]{:S(2)}) async-start(), calls=%async_computation.3 | async-start | bytes 4128768 | tf_op jit(solution)/shard_map/all_gather | solution.py:54
  165.6 45.8 %copy-start.4 = (bf16[64,512]{1,0:T(8,128)(2,1)S(1)}, bf16[64,512]{1,0:T(8,128)(2,1)}, u32[]{:S(2)}) copy-start(bf16[64,512]{1,0:T(8,128)(2,1)} %param.21) | copy-start | bytes 196612
  165.6 73.2 %copy-start.3 = (bf16[64,1024]{1,0:T(8,128)(2,1)S(1)}, bf16[64,1024]{1,0:T(8,128)(2,1)}, u32[]{:S(2)}) copy-start(bf16[64,1024]{1,0:T(8,128)(2,1)} %param.14) | copy-start | bytes 393220
  165.6 87.5 %copy-start.6 = (f32[1024]{0:T(1024)S(1)}, f32[1024]{0:T(1024)}, u32[]{:S(2)}) copy-start(f32[1024]{0:T(1024)} %param.19) | copy-start | bytes 12292
  165.6 89.3 %copy-start.7 = (f32[512]{0:T(512)S(1)}, f32[512]{0:T(512)}, u32[]{:S(2)}) copy-start(f32[512]{0:T(512)} %param.22) | copy-start | bytes 6148
  165.6 73.2 %reduce-scatter.5.cloned.1.call-start = ((), (), s32[]{:S(2)}) async-start(), calls=%async_computation.4 | async-start | bytes 1310720 | tf_op jit(solution)/shard_map/reduce_scatter | solution.py:58
  211.3 64.1 %copy-start.8 = (s32[256]{0:T(256)S(1)}, s32[256]{0:T(256)}, u32[]{:S(2)}) copy-start(s32[256]{0:T(256)} %param.25) | copy-start | bytes 3076
  211.3 64.9 %copy-start.5 = (s32[2048]{0:T(1024)S(1)}, s32[2048]{0:T(1024)}, u32[]{:S(2)}) copy-start(s32[2048]{0:T(1024)} %param.27) | copy-start | bytes 24580
  211.4 111.2 %copy-start.9 = (f32[256]{0:T(256)S(1)}, f32[256]{0:T(256)}, u32[]{:S(2)}) copy-start(f32[256]{0:T(256)} %param.24) | copy-start | bytes 3076
  211.4 64.0 %all-gather.7.cloned.1.call-start = ((), (), s32[]{:S(2)}) async-start(), calls=%async_computation.5 | async-start | bytes 1179648 | tf_op jit(solution)/shard_map/all_gather | solution.py:66
  254.8 67.7 %all-gather.11.cloned.1.call-start = ((), (), s32[]{:S(2)}) async-start(), calls=%async_computation.7 | async-start | bytes 2621440 | tf_op jit(solution)/shard_map/all_gather | solution.py:71
  265.6 138.0 %all-gather.9.cloned.1.call-start = ((), (), s32[]{:S(2)}) async-start(), calls=%async_computation.6 | async-start | bytes 5242880 | tf_op jit(solution)/shard_map/all_gather | solution.py:70
  502.1 43.8 %copy-start.1 = (s32[8,24]{1,0:T(8,128)S(1)}, s32[8,24]{1,0:T(8,128)}, u32[]{:S(2)}) copy-start(s32[8,24]{1,0:T(8,128)} %param.26) | copy-start | bytes 2308
Sparse Core Ops, SparseCore 0:
  59.4 103.6 reduce-scatter.2
  165.7 34.3 all-gather.4
  211.5 27.2 reduce-scatter.4
  255.0 20.3 all-gather.6
  276.8 45.6 all-gather.10
  323.9 79.5 all-gather.8
where the time goes:
time: 553 us
  waiting for transfers between devices  273 us (49%)
  blocking collectives  173 us (31%)
  matrix products  48.7 us (9%)
  other arithmetic  40.4 us (7%)
  between operations  14.3 us (3%)
    reduce_scatter x1, waiting for transfers between devices, body(): lax.psum_scatter(both_halves(rows_exp, exp_gate, exp_up), 'tp', scatter_d...  104 us
    all_gather x1, waiting for transfers between devices, body(): lax.all_gather(features_exp, 'rep', axis=0, tiled=True)  72.2 us
    psum x1, blocking collectives, body(): total_exp, total_ama = lax.psum((local_exp, local_ama), ('rep', 'tp'))  40.4 us
    pmax x1, blocking collectives, body(): beam_best = lax.pmax(jnp.max(scores, axis=1), ('rep', 'tp'))  39.4 us
    pmax x1, blocking collectives, body(): lax.pmax((jnp.max(logits_exp, axis=1), jnp.max(logits_ama, axis=1)), ('re...  38.6 us
    all_gather x1, waiting for transfers between devices, body(): lax.all_gather(hidden_exp, 'tp', axis=0, tiled=True)  34.4 us
    reduce_scatter x1, waiting for transfers between devices, body(): out_exp = lax.psum_scatter(term_exp, 'rep', scatter_dimension=0, tiled=True)  27.3 us
    all_gather x1, waiting for transfers between devices, body(): lax.all_gather(features_ama, 'rep', axis=0, tiled=True)  25.5 us
  transfers between devices with their start and end apart: 6, of which 6 were waited for; matrix products, arithmetic and copies ran while one was open for 6% of the time, Pallas kernels for 0%

commit v1 on v0

--- a/solution.py
+++ b/solution.py
@@ -8,6 +8,19 @@
 norm_epsilon = 1e-05
 contrast_weight = 0.5
 hamming_weight = 0.7
+
+
+def gather_around(shard, axis, dim):
+    devices, index, width = (lax.axis_size(axis), lax.axis_index(axis), shard.shape[dim])
+    upward = [(i, (i + 1) % devices) for i in range(devices)]
+    out = jnp.zeros((*shard.shape[:dim], devices * width, *shard.shape[dim + 1 :]), shard.dtype)
+    held = shard
+    for step in range(devices):
+        owner = (index - step) % devices
+        out = lax.dynamic_update_slice_in_dim(out, held, owner * width, axis=dim)
+        if step < devices - 1:
+            held = lax.ppermute(held, axis, upward)
+    return out
 
 
 def scaled_rows(values, squares, width, gain):
@@ -51,9 +64,7 @@
     )
     hidden_exp = gated_rows(summed_exp, width_exp)
     term_exp = jnp.dot(
-        lax.all_gather(hidden_exp, "tp", axis=0, tiled=True),
-        exp_down,
-        preferred_element_type=jnp.float32,
+        gather_around(hidden_exp, "tp", 0), exp_down, preferred_element_type=jnp.float32
     )
     out_exp = lax.psum_scatter(term_exp, "rep", scatter_dimension=0, tiled=True)
     layer_exp = values_exp + out_exp

time: 553 us -> 582 us (1.052)
  waiting for transfers between devices: 273 us -> 295 us
  local copies, waits for them, and re-layouts: 2.73 us -> 10.6 us
    ppermute x0 -> x7, waiting for transfers between devices: none -> 56.7 us  [gather_around(): held = lax.ppermute(held, axis, upward)]
    all_gather x1 -> x0, waiting for transfers between devices: 34.4 us -> none  [body(): lax.all_gather(hidden_exp, 'tp', axis=0, tiled=True)]
  transfers between devices with their start and end apart: 6 -> 12, of which waited for: 6 -> 12; matrix products, arithmetic and copies ran while one was open for 6% -> 6% of each run, Pallas kernels for 0% -> 0%
where the time goes in v1:
time: 582 us; the launch traced here: 581 us
  waiting for transfers between devices  295 us (51%)
  blocking collectives  173 us (30%)
  matrix products  48.7 us (8%)
  other arithmetic  39 us (7%)
  between operations  14 us (2%)
  local copies, waits for them, and re-layouts  10.6 us (2%)
    reduce_scatter x1, waiting for transfers between devices, body(): lax.psum_scatter(both_halves(rows_exp, exp_gate, exp_up), 'tp', scatter_d...  104 us
    all_gather x1, waiting for transfers between devices, body(): lax.all_gather(features_exp, 'rep', axis=0, tiled=True)  72.2 us
    ppermute x7, waiting for transfers between devices, gather_around(): held = lax.ppermute(held, axis, upward)  56.7 us
    psum x1, blocking collectives, body(): total_exp, total_ama = lax.psum((local_exp, local_ama), ('rep', 'tp'))  40.4 us
    pmax x1, blocking collectives, body(): beam_best = lax.pmax(jnp.max(scores, axis=1), ('rep', 'tp'))  39.4 us
    pmax x1, blocking collectives, body(): lax.pmax((jnp.max(logits_exp, axis=1), jnp.max(logits_ama, axis=1)), ('re...  38.6 us
    reduce_scatter x1, waiting for transfers between devices, body(): out_exp = lax.psum_scatter(term_exp, 'rep', scatter_dimension=0, tiled=True)  27.3 us
    all_gather x1, waiting for transfers between devices, body(): lax.all_gather(features_ama, 'rep', axis=0, tiled=True)  25.5 us
  transfers between devices with their start and end apart: 12, of which 12 were waited for; matrix products, arithmetic and copies ran while one was open for 6% of the time, Pallas kernels for 0%

profile of v1, /device:TPU:0, one launch (start us, length us, event | category | flops | bytes accessed | tf_op | source)
XLA Modules:
  0.0 581.1 jit_solution(13912002577094385289)
XLA Ops:
  7.2 1.0 fusion.1
  8.3 15.2 %psum.35 = f32[64]{0:T(128)S(1)} all-reduce(f32[64]{0:T(128)S(1)} %fusion.1), channel_id=1, replica_groups=mesh['rep'=4,'tp'=8] {'tp'}, use_global_device_ids=true, to_apply=%region_1.0 | all-reduce | flops 64 | bytes 512 | tf_op jit(solution)/shard_map/psum | solution.py:58
  23.4 1.0 fusion.3
  24.4 15.9 %all_gather.15 = bf16[256,1024]{1,0:T(8,128)(2,1)S(1)} all-gather(bf16[64,1024]{1,0:T(8,128)(2,1)S(1)} %fusion.3), channel_id=1, replica_groups=mesh['rep'=4,'tp'=8] {'rep'}, dimensions={0}, use_global_device_ids=true | all-gather | bytes 655360 | tf_op jit(solution)/shard_map/all_gather | solution.py:60
  40.4 7.4 %fusion.11 = f32[256,7168]{1,0:T(8,128)S(1)} fusion(bf16[256,1024]{1,0:T(8,128)(2,1)S(1)} %all_gather.15, bf16[1024,7168]{1,0:T(8,128)(2,1)} %param.16), kind=kOutput, calls=%fused_computation.43 | convolution fusion | flops 3758096384 | bytes 22544384 | tf_op jit(solution)/shard_map/dot_general | solution.py:31
  47.8 1.9 copy-done.2
  49.7 4.1 fusion.12
  53.8 5.5 pad_maximum_fusion
  59.4 103.7 %reduce-scatter.3.cloned.1.call-done = f32[32,14336]{1,0:T(8,128)} async-done(((f32[256,14336]{1,0:T(8,128)}), f32[32,14336]{1,0:T(8,128)}) %reduce-scatter.3.cloned.1.call-update) | async-done | bytes 1835024 | tf_op jit(solution)/shard_map/reduce_scatter | solution.py:62
  163.1 2.2 broadcast_in_dim.11
  165.3 1.0 constant_dynamic-update-slice_fusion.7
  166.3 8.8 %collective-permute-done = bf16[32,7168]{1,0:T(8,128)(2,1)S(1)} collective-permute-done((bf16[32,7168]{1,0:T(8,128)(2,1)S(1)}, bf16[32,7168]{1,0:T(8,128)(2,1)S(1)}, u32[]{:S(2)}, u32[]{:S(2)}) %collective-permute-start) | collective-permute-done | bytes 458784 | tf_op jit(solution)/shard_map/ppermute | solution.py:22
  175.1 0.8 constant_dynamic-update-slice_fusion.6
  175.9 8.0 %collective-permute-done.1 = bf16[32,7168]{1,0:T(8,128)(2,1)S(1)} collective-permute-done((bf16[32,7168]{1,0:T(8,128)(2,1)S(1)}, bf16[32,7168]{1,0:T(8,128)(2,1)S(1)}, u32[]{:S(2)}, u32[]{:S(2)}) %collective-permute-start.1) | collective-permute-done | bytes 458784 | tf_op jit(solution)/shard_map/ppermute | solution.py:22
  183.9 0.8 constant_dynamic-update-slice_fusion.5
  184.8 8.0 %collective-permute-done.2 = bf16[32,7168]{1,0:T(8,128)(2,1)S(1)} collective-permute-done((bf16[32,7168]{1,0:T(8,128)(2,1)S(1)}, bf16[32,7168]{1,0:T(8,128)(2,1)S(1)}, u32[]{:S(2)}, u32[]{:S(2)}) %collective-permute-start.2) | collective-permute-done | bytes 458784 | tf_op jit(solution)/shard_map/ppermute | solution.py:22
  192.7 0.8 constant_dynamic-update-slice_fusion.4
  193.5 8.0 %collective-permute-done.3 = bf16[32,7168]{1,0:T(8,128)(2,1)S(1)} collective-permute-done((bf16[32,7168]{1,0:T(8,128)(2,1)S(1)}, bf16[32,7168]{1,0:T(8,128)(2,1)S(1)}, u32[]{:S(2)}, u32[]{:S(2)}) %collective-permute-start.3) | collective-permute-done | bytes 458784 | tf_op jit(solution)/shard_map/ppermute | solution.py:22
  201.5 0.8 constant_dynamic-update-slice_fusion.3
  202.3 8.0 %collective-permute-done.4 = bf16[32,7168]{1,0:T(8,128)(2,1)S(1)} collective-permute-done((bf16[32,7168]{1,0:T(8,128)(2,1)S(1)}, bf16[32,7168]{1,0:T(8,128)(2,1)S(1)}, u32[]{:S(2)}, u32[]{:S(2)}) %collective-permute-start.4) | collective-permute-done | bytes 458784 | tf_op jit(solution)/shard_map/ppermute | solution.py:22
  210.3 0.8 constant_dynamic-update-slice_fusion.2
  211.2 8.0 %collective-permute-done.5 = bf16[32,7168]{1,0:T(8,128)(2,1)S(1)} collective-permute-done((bf16[32,7168]{1,0:T(8,128)(2,1)S(1)}, bf16[32,7168]{1,0:T(8,128)(2,1)S(1)}, u32[]{:S(2)}, u32[]{:S(2)}) %collective-permute-start.5) | collective-permute-done | bytes 458784 | tf_op jit(solution)/shard_map/ppermute | solution.py:22
  219.1 0.8 constant_dynamic-update-slice_fusion.1
  220.0 8.0 %collective-permute-done.6 = bf16[32,7168]{1,0:T(8,128)(2,1)S(1)} collective-permute-done((bf16[32,7168]{1,0:T(8,128)(2,1)S(1)}, bf16[32,7168]{1,0:T(8,128)(2,1)S(1)}, u32[]{:S(2)}, u32[]{:S(2)}) %collective-permute-start.6) | collective-permute-done | bytes 458784 | tf_op jit(solution)/shard_map/ppermute | solution.py:22
  227.9 0.8 constant_dynamic-update-slice_fusion
  228.8 11.2 %fusion.13 = f32[256,1024]{1,0:T(8,128)} fusion(bf16[256,7168]{1,0:T(8,128)(2,1)} %constant_dynamic-update-slice_fusion, bf16[7168,1024]{1,0:T(8,128)(2,1)} %param.18), kind=kOutput, calls=%fused_computation.45 | convolution fusion | flops 3758096384 | bytes 19398656 | tf_op jit(solution)/shard_map/dot_general | solution.py:66
  240.1 0.0 all-gather.4.cloned.1.call-start
  240.1 0.1 fusion.4
  240.2 27.3 %reduce-scatter.5.cloned.1.call-done = f32[64,1024]{1,0:T(8,128)} async-done(((f32[256,1024]{1,0:T(8,128)}), f32[64,1024]{1,0:T(8,128)}) %reduce-scatter.5.cloned.1.call-update) | async-done | bytes 262160 | tf_op jit(solution)/shard_map/reduce_scatter | solution.py:69
  267.5 1.1 multiply_reduce_fusion
  268.6 13.2 %all-reduce.2 = (f32[64]{0:T(128)S(1)}, f32[64]{0:T(128)S(1)}) all-reduce(f32[64]{0:T(128)S(1)} %fusion.4, f32[64]{0:T(128)S(1)} %multiply_reduce_fusion), channel_id=1, replica_groups=mesh['rep'=4,'tp'=8] {'tp'}, use_global_device_ids=true, to_apply=%region_11.12 | all-reduce | flops 128 | bytes 1024 | tf_op jit(solution)/shard_map/psum | solution.py:71
  281.8 1.7 multiply_convert_fusion
  283.6 0.1 fusion.6
  283.7 10.5 %all_gather.18 = bf16[64,4096]{1,0:T(8,128)(2,1)} all-gather(bf16[64,512]{1,0:T(8,128)(2,1)S(1)} %fusion.6), channel_id=1, replica_groups=mesh['rep'=4,'tp'=8] {'tp'}, dimensions={1}, use_global_device_ids=true | all-gather | bytes 589824 | tf_op jit(solution)/shard_map/all_gather | solution.py:78
  294.2 0.2 all-gather.6.cloned.1.call-start
  294.5 9.6 %all-gather.4.cloned.1.call-done = bf16[64,8192]{1,0:T(8,128)(2,1)} async-done(((bf16[64,1024]{1,0:T(8,128)(2,1)}), bf16[64,8192]{1,0:T(8,128)(2,1)}) %all-gather.4.cloned.1.call-update) | async-done | bytes 1048592 | tf_op jit(solution)/shard_map/all_gather | solution.py:77
  304.2 0.7 gather_fusion
  304.9 0.1 broadcast_select_fusion
  305.1 20.6 %convert_reduce_fusion = f32[256,2048]{1,0:T(8,128)} fusion(s32[2048]{0:T(1024)S(1)} %iota_add_fusion, s32[256,24]{1,0:T(8,128)S(1)} %broadcast_select_fusion), kind=kLoop, calls=%fused_computation.1 | loop fusion | flops 37224448 | bytes 2129920 | tf_op jit(solution)/shard_map/reduce_sum | solution.py:102
  325.7 25.5 %all-gather.8.cloned.1.call-done = bf16[256,4096]{1,0:T(8,128)(2,1)} async-done(((bf16[64,4096]{1,0:T(8,128)(2,1)}), bf16[256,4096]{1,0:T(8,128)(2,1)}) %all-gather.8.cloned.1.call-update) | async-done | bytes 2097168 | tf_op jit(solution)/shard_map/all_gather | solution.py:82
  351.2 8.8 %fusion.9 = (f32[256]{0:T(256)S(1)}, f32[256,2048]{1,0:T(8,128)S(1)}) fusion(bf16[256,4096]{1,0:T(8,128)(2,1)} %all-gather.8.cloned.1.call-done, bf16[4096,2048]{1,0:T(8,128)(2,1)} %param.23, f32[256]{0:T(256)S(1)} %copy-done.10), kind=kOutput, calls=%fused_computation.41 | convolution fusion | flops 4296015872 | bytes 20973568 | tf_op jit(solution)/shard_map/dot_general | solution.py:87
  360.0 72.2 %all-gather.6.cloned.1.call-done = bf16[256,8192]{1,0:T(8,128)(2,1)} async-done(((bf16[64,8192]{1,0:T(8,128)(2,1)}), bf16[256,8192]{1,0:T(8,128)(2,1)}) %all-gather.6.cloned.1.call-update) | async-done | bytes 4194320 | tf_op jit(solution)/shard_map/all_gather | solution.py:81
  432.2 17.2 %fusion.10 = (f32[256]{0:T(256)S(1)}, f32[256,2048]{1,0:T(8,128)}) fusion(bf16[256,8192]{1,0:T(8,128)(2,1)} %all-gather.6.cloned.1.call-done, bf16[8192,2048]{1,0:T(8,128)(2,1)} %param.20, f32[256]{0:T(256)S(1)} %copy-done.10), kind=kOutput, calls=%fused_computation.42 | convolution fusion | flops 8590983168 | bytes 39847936 | tf_op jit(solution)/shard_map/dot_general | solution.py:84
  449.4 38.6 %all-reduce.1 = (f32[256]{0:T(256)S(1)}, f32[256]{0:T(256)S(1)}) all-reduce(f32[256]{0:T(256)S(1)} %get-tuple-element.12, f32[256]{0:T(256)S(1)} %get-tuple-element.14), channel_id=1, replica_groups=mesh['rep'=4,'tp'=8] {'rep','tp'}, use_global_device_ids=true, to_apply=%region_13.14 | all-reduce | flops 512 | bytes 4096 | tf_op jit(solution)/shard_map/pmax | solution.py:90
  488.1 2.3 exponential_reduce_fusion
  490.3 40.4 %all-reduce = (f32[256]{0:T(256)S(1)}, f32[256]{0:T(256)S(1)}) all-reduce(f32[256]{0:T(256)S(1)} %get-tuple-element.16, f32[256]{0:T(256)S(1)} %get-tuple-element.17), channel_id=1, replica_groups=mesh['rep'=4,'tp'=8] {'rep','tp'}, use_global_device_ids=true, to_apply=%region_15.16 | all-reduce | flops 512 | bytes 4096 | tf_op jit(solution)/shard_map/psum | solution.py:95
  530.8 4.4 fusion.7
  535.2 39.4 %pmax.23 = f32[256]{0:T(256)} all-reduce(f32[256]{0:T(256)S(1)} %get-tuple-element.8), channel_id=1, replica_groups=mesh['rep'=4,'tp'=8] {'rep','tp'}, use_global_device_ids=true, to_apply=%region_18.19 | all-reduce | flops 256 | bytes 2048 | tf_op jit(solution)/shard_map/pmax | solution.py:107
  (46 shorter events, 0.3 us)
Async XLA Ops:
  7.2 297.0 %copy-start = (s32[8,24]{1,0:T(8,128)S(1)}, s32[8,24]{1,0:T(8,128)}, u32[]{:S(2)}) copy-start(s32[8,24]{1,0:T(8,128)} %param.26) | copy-start | bytes 2308
  7.2 155.9 %reduce-scatter.3.cloned.1.call-start = ((), (), s32[]{:S(2)}) async-start(), calls=%async_computation.2 | async-start | bytes 16515072 | tf_op jit(solution)/shard_map/reduce_scatter | solution.py:62
  40.4 9.3 %copy-start.2 = (bf16[1024,7168]{1,0:T(8,128)(2,1)S(1)}, bf16[1024,7168]{1,0:T(8,128)(2,1)}, u32[]{:S(2)}) copy-start(bf16[1024,7168]{1,0:T(8,128)(2,1)} %param.17) | copy-start | bytes 44040196
  59.3 208.2 %reduce-scatter.5.cloned.1.call-start = ((), (), s32[]{:S(2)}) async-start(), calls=%async_computation.3 | async-start | bytes 1310720 | tf_op jit(solution)/shard_map/reduce_scatter | solution.py:69
  163.1 2.2 copy-start.4
  166.3 8.8 %collective-permute-start = (bf16[32,7168]{1,0:T(8,128)(2,1)S(1)}, bf16[32,7168]{1,0:T(8,128)(2,1)S(1)}, u32[]{:S(2)}, u32[]{:S(2)}) collective-permute-start(bf16[32,7168]{1,0:T(8,128)(2,1)S(1)} %get-tuple-element.11), channel_id=1, source_target_pairs={{0,1},{1,2},{2,3},{3,4},{4,5},{5,6},{6,7},{7,0},{8,9},{9,10},{10,1... | collective-permute-start | bytes 1376264 | tf_op jit(solution)/shard_map/ppermute | solution.py:22
  175.1 8.8 %collective-permute-start.1 = (bf16[32,7168]{1,0:T(8,128)(2,1)S(1)}, bf16[32,7168]{1,0:T(8,128)(2,1)S(1)}, u32[]{:S(2)}, u32[]{:S(2)}) collective-permute-start(bf16[32,7168]{1,0:T(8,128)(2,1)S(1)} %collective-permute-done), channel_id=1, source_target_pairs={{0,1},{1,2},{2,3},{3,4},{4,5},{5,6},{6,7},{7,0},{8,9},{9,10},{10,1... | collective-permute-start | bytes 1376264 | tf_op jit(solution)/shard_map/ppermute | solution.py:22
  183.9 8.8 %collective-permute-start.2 = (bf16[32,7168]{1,0:T(8,128)(2,1)S(1)}, bf16[32,7168]{1,0:T(8,128)(2,1)S(1)}, u32[]{:S(2)}, u32[]{:S(2)}) collective-permute-start(bf16[32,7168]{1,0:T(8,128)(2,1)S(1)} %collective-permute-done.1), channel_id=1, source_target_pairs={{0,1},{1,2},{2,3},{3,4},{4,5},{5,6},{6,7},{7,0},{8,9},{9,10},{10,1... | collective-permute-start | bytes 1376264 | tf_op jit(solution)/shard_map/ppermute | solution.py:22
  192.7 8.8 %collective-permute-start.3 = (bf16[32,7168]{1,0:T(8,128)(2,1)S(1)}, bf16[32,7168]{1,0:T(8,128)(2,1)S(1)}, u32[]{:S(2)}, u32[]{:S(2)}) collective-permute-start(bf16[32,7168]{1,0:T(8,128)(2,1)S(1)} %collective-permute-done.2), channel_id=1, source_target_pairs={{0,1},{1,2},{2,3},{3,4},{4,5},{5,6},{6,7},{7,0},{8,9},{9,10},{10,1... | collective-permute-start | bytes 1376264 | tf_op jit(solution)/shard_map/ppermute | solution.py:22
  201.5 8.8 %collective-permute-start.4 = (bf16[32,7168]{1,0:T(8,128)(2,1)S(1)}, bf16[32,7168]{1,0:T(8,128)(2,1)S(1)}, u32[]{:S(2)}, u32[]{:S(2)}) collective-permute-start(bf16[32,7168]{1,0:T(8,128)(2,1)S(1)} %collective-permute-done.3), channel_id=1, source_target_pairs={{0,1},{1,2},{2,3},{3,4},{4,5},{5,6},{6,7},{7,0},{8,9},{9,10},{10,1... | collective-permute-start | bytes 1376264 | tf_op jit(solution)/shard_map/ppermute | solution.py:22
  210.3 8.8 %collective-permute-start.5 = (bf16[32,7168]{1,0:T(8,128)(2,1)S(1)}, bf16[32,7168]{1,0:T(8,128)(2,1)S(1)}, u32[]{:S(2)}, u32[]{:S(2)}) collective-permute-start(bf16[32,7168]{1,0:T(8,128)(2,1)S(1)} %collective-permute-done.4), channel_id=1, source_target_pairs={{0,1},{1,2},{2,3},{3,4},{4,5},{5,6},{6,7},{7,0},{8,9},{9,10},{10,1... | collective-permute-start | bytes 1376264 | tf_op jit(solution)/shard_map/ppermute | solution.py:22
  219.1 8.8 %collective-permute-start.6 = (bf16[32,7168]{1,0:T(8,128)(2,1)S(1)}, bf16[32,7168]{1,0:T(8,128)(2,1)S(1)}, u32[]{:S(2)}, u32[]{:S(2)}) collective-permute-start(bf16[32,7168]{1,0:T(8,128)(2,1)S(1)} %collective-permute-done.5), channel_id=1, source_target_pairs={{0,1},{1,2},{2,3},{3,4},{4,5},{5,6},{6,7},{7,0},{8,9},{9,10},{10,1... | collective-permute-start | bytes 1376264 | tf_op jit(solution)/shard_map/ppermute | solution.py:22
  228.8 11.3 %copy-start.5 = (bf16[64,512]{1,0:T(8,128)(2,1)S(1)}, bf16[64,512]{1,0:T(8,128)(2,1)}, u32[]{:S(2)}) copy-start(bf16[64,512]{1,0:T(8,128)(2,1)} %param.21) | copy-start | bytes 196612
  228.8 38.7 %copy-start.3 = (bf16[64,1024]{1,0:T(8,128)(2,1)S(1)}, bf16[64,1024]{1,0:T(8,128)(2,1)}, u32[]{:S(2)}) copy-start(bf16[64,1024]{1,0:T(8,128)(2,1)} %param.14) | copy-start | bytes 393220
  228.8 53.0 %copy-start.7 = (f32[1024]{0:T(1024)S(1)}, f32[1024]{0:T(1024)}, u32[]{:S(2)}) copy-start(f32[1024]{0:T(1024)} %param.19) | copy-start | bytes 12292
  228.8 54.8 %copy-start.8 = (f32[512]{0:T(512)S(1)}, f32[512]{0:T(512)}, u32[]{:S(2)}) copy-start(f32[512]{0:T(512)} %param.22) | copy-start | bytes 6148
  240.0 64.1 %copy-start.9 = (s32[256]{0:T(256)S(1)}, s32[256]{0:T(256)}, u32[]{:S(2)}) copy-start(s32[256]{0:T(256)} %param.25) | copy-start | bytes 3076
  240.0 64.9 %copy-start.6 = (s32[2048]{0:T(1024)S(1)}, s32[2048]{0:T(1024)}, u32[]{:S(2)}) copy-start(s32[2048]{0:T(1024)} %param.27) | copy-start | bytes 24580
  240.0 111.2 %copy-start.10 = (f32[256]{0:T(256)S(1)}, f32[256]{0:T(256)}, u32[]{:S(2)}) copy-start(f32[256]{0:T(256)} %param.24) | copy-start | bytes 3076
  240.1 64.0 %all-gather.4.cloned.1.call-start = ((), (), s32[]{:S(2)}) async-start(), calls=%async_computation.4 | async-start | bytes 1179648 | tf_op jit(solution)/shard_map/all_gather | solution.py:77
  283.5 67.7 %all-gather.8.cloned.1.call-start = ((), (), s32[]{:S(2)}) async-start(), calls=%async_computation.6 | async-start | bytes 2621440 | tf_op jit(solution)/shard_map/all_gather | solution.py:82
  294.2 138.0 %all-gather.6.cloned.1.call-start = ((), (), s32[]{:S(2)}) async-start(), calls=%async_computation.5 | async-start | bytes 5242880 | tf_op jit(solution)/shard_map/all_gather | solution.py:81
  530.8 43.8 %copy-start.1 = (s32[8,24]{1,0:T(8,128)S(1)}, s32[8,24]{1,0:T(8,128)}, u32[]{:S(2)}) copy-start(s32[8,24]{1,0:T(8,128)} %param.26) | copy-start | bytes 2308
Sparse Core Ops, SparseCore 0:
  59.4 103.6 reduce-scatter.2
  240.2 27.2 reduce-scatter.4
  283.6 20.4 all-gather.3
  305.5 45.6 all-gather.7
  352.6 79.5 all-gather.5
